TPU v7x, 32 devices: a whole 2x2x4 slice. The times are simulated.
32 devices in a mesh: lat: 16 (over z, x, core), lev: 2 (over y).
Axes of the slice: x: 2, y: 2, z: 4, core: 2. Of those that a mesh axis runs over, the one named last changes fastest.
Arguments:
- anomalies: bfloat16 [4, 2, 80, 32, 1536], P(None, 'lev', None, 'lat'), may hold values from -6 to 6
- error_now: float32 [4, 2, 32, 1536], P(None, 'lev', 'lat'), may hold values from -6 to 6
- error_prior: float32 [4, 2, 32, 1536], P(None, 'lev', 'lat'), may hold values from -4.2 to 4.2
- energy_coef: float32 [4, 2], P(None, 'lev'), may hold values from 0.3 to 3
- obs_anomalies: bfloat16 [2048, 80, 256], P('lat', 'lev'), may hold values from -6 to 6
- innovations: float32 [2048, 256], P('lat'), may hold values from -6 to 6
- valid_counts: int32 [2048], P('lat'), may hold values from 0 to 256, as said below
- type_ids: int32 [2048], P('lat'), may hold values from 0 to 7
- error_inverse: float32 [8], replicated, may hold values from 0.25 to 4
Outputs:
- impact: float32 [2048, 16, 256], P('lat', 'lev')
- type_totals: float32 [16, 8], P('lev')
Inputs may be any that keep to these rules, and one draw needn't show every extreme that they name: `valid_counts`: among the 128 slots of each index of lat, the blocks with a positive count come first and the first is always positive; in every draw some index of lat has all 128 slots positive and some block holds 256 rows. Rows below a block's count are observations, the rest padding.
All inputs are finite; a program needn't handle non-finite values.
Results may differ from a plain program's by a relative error of at most 0.0042.
Values may be sent and summed in bfloat16 or wider, within the bound.
No kernel may reach another device: no remote copies, remote signals or barrier semaphores. Data moves between devices by JAX's collectives and lax.ppermute only.
A program may use at most 64 MiB of HBM per device.

v0:
```python
import math
import jax
import jax.numpy as jnp
from jax import lax
from jax.sharding import PartitionSpec as P

NLAT_GRID = 768
LAT0 = 256
REGIONS = 4
NTYPES = 8


def local(
    anomalies,
    error_now,
    error_prior,
    energy_coef,
    obs_anomalies,
    innovations,
    valid_counts,
    type_ids,
    error_inverse,
):
    lat_rows = error_now.shape[2]
    lat_total = lat_rows * lax.axis_size("lat")
    lev_total = error_now.shape[1] * lax.axis_size("lev")
    lon_count = error_now.shape[3]
    lat_index = lax.axis_index("lat") * lat_rows + jnp.arange(lat_rows, dtype=jnp.int32)
    cosine = jnp.cos(
        -0.5 * math.pi + ((lat_index + LAT0).astype(jnp.float32) + 0.5) * math.pi / NLAT_GRID
    )
    gradient = (
        energy_coef[:, :, None, None] * cosine[None, None, :, None] * (error_now + error_prior)
    ).astype(jnp.bfloat16)
    folded = jnp.einsum("vlkji,vlji->vkj", anomalies, gradient, preferred_element_type=jnp.float32)
    region = lat_index * REGIONS // lat_total
    onehot = (region[None, :] == jnp.arange(REGIONS, dtype=jnp.int32)[:, None]).astype(jnp.float32)
    partial_value = jnp.einsum("vkj,rj->vkr", folded, onehot, precision=lax.Precision.HIGHEST)
    summed = lax.psum(partial_value, ("lat", "lev"))
    members = anomalies.shape[2]
    norm_scale = math.sqrt(lev_total * lat_total * lon_count / REGIONS)
    weights = (jnp.transpose(summed, (1, 0, 2)).reshape(members, -1) / norm_scale).astype(
        jnp.bfloat16
    )
    slot_count, local_members, block_rows = obs_anomalies.shape
    lev_groups = lax.axis_size("lev")
    grouped = obs_anomalies.reshape(lev_groups, slot_count // lev_groups, local_members, block_rows)
    answered = jnp.einsum(
        "gbks,kt->gbts",
        lax.all_to_all(grouped, "lev", split_axis=0, concat_axis=2, tiled=True),
        weights,
        preferred_element_type=jnp.float32,
    )
    response = lax.all_to_all(answered[0], "lev", split_axis=1, concat_axis=0, tiled=True)
    type_table = type_ids[:, None] == jnp.arange(NTYPES, dtype=jnp.int32)[None, :]
    inverse_var = jnp.sum(
        jnp.where(type_table, error_inverse[None, :], jnp.zeros((), jnp.float32)), axis=1
    )
    positions = jnp.arange(block_rows, dtype=jnp.int32)
    row_mask = (positions[None, :] < valid_counts[:, None]).astype(jnp.float32)
    scaling = innovations * inverse_var[:, None] * row_mask / math.sqrt(members - 1)
    impact = response * scaling[:, None, :]
    per_block = jnp.sum(impact, axis=2)
    local_totals = jnp.dot(
        per_block.T, type_table.astype(jnp.float32), precision=lax.Precision.HIGHEST
    )
    block_total = slot_count * lax.axis_size("lat")
    type_totals = lax.psum(local_totals, "lat") / math.sqrt(block_total * block_rows / NTYPES)
    return (impact, type_totals)


def solution(mesh):
    in_specs = (
        P(None, "lev", None, "lat", None),
        P(None, "lev", "lat", None),
        P(None, "lev", "lat", None),
        P(None, "lev"),
        P("lat", "lev", None),
        P("lat", None),
        P("lat"),
        P("lat"),
        P(),
    )
    out_specs = (P("lat", "lev", None), P("lev", None))
    return jax.shard_map(local, mesh=mesh, in_specs=in_specs, out_specs=out_specs, check_vma=False)
```

profile of v0, /device:TPU:0, one launch (start us, length us, event | category | flops | bytes accessed | tf_op | source)
XLA Modules:
  0.0 126.0 jit_solution(2320645867197905039)
XLA Ops:
  0.6 0.0 copy-start
  0.7 5.2 %all-to-all-start = ((bf16[2,64,40,256]{3,2,1,0:T(8,128)(2,1)}), bf16[2,64,40,256]{3,2,1,0:T(8,128)(2,1)}, u32[]{:S(2)}, u32[]{:S(2)}) async-start(bf16[2,64,40,256]{3,2,1,0:T(8,128)(2,1)} %bitcast.48), calls=%async_computation | async-start | bytes 5242880 | tf_op jit(solution)/shard_map/all_to_all | solution.py:50
  5.9 0.1 broadcast_multiply_fusion.1
  6.0 0.1 fusion.4
  6.1 0.6 fusion
  6.7 0.3 fusion.7
  7.0 65.6 %psum.14 = f32[4,80,4]{1,2,0:T(4,128)S(1)} all-reduce(f32[4,80,4]{1,2,0:T(4,128)S(1)} %fusion.7), channel_id=1, replica_groups=mesh['lat'=16,'lev'=2] {'lat','lev'}, use_global_device_ids=true, to_apply=%region_0.1 | all-reduce | flops 1280 | bytes 10240 | tf_op jit(solution)/shard_map/psum | solution.py:39
  72.5 1.9 %copy.25 = bf16[1,64,2,40,256]{4,3,2,1,0:T(8,128)(2,1)S(1)} copy(bf16[1,64,2,40,256]{4,3,1,2,0:T(8,128)(2,1)} %bitcast.13) | data formatting | bytes 5242880 | tf_op jit(solution)/shard_map/all_to_all | solution.py:50
  74.5 0.5 convolution_bitcast_fusion
  75.0 0.0 copy-start.4
  75.0 1.6 %copy.26 = f32[64,16,256]{2,0,1:T(8,128)} copy(f32[64,16,256]{2,1,0:T(8,128)S(1)} %convolution_bitcast_fusion) | data formatting | bytes 2097152 | tf_op jit(solution)/shard_map/squeeze | solution.py:54
  76.6 3.6 %all-to-all-start.1 = ((f32[64,16,256]{2,0,1:T(8,128)}), f32[64,16,256]{2,0,1:T(8,128)S(1)}, u32[]{:S(2)}, u32[]{:S(2)}) async-start(f32[64,16,256]{2,0,1:T(8,128)} %copy.26), calls=%async_computation.1 | async-start | bytes 2097152 | tf_op jit(solution)/shard_map/all_to_all | solution.py:54
  80.2 0.1 select_reduce_fusion
  80.3 0.1 select_multiply_fusion
  80.4 0.1 copy.29
  80.5 12.7 %all-to-all-done.1 = f32[64,16,256]{2,0,1:T(8,128)S(1)} async-done(((f32[64,16,256]{2,0,1:T(8,128)}), f32[64,16,256]{2,0,1:T(8,128)S(1)}, u32[]{:S(2)}, u32[]{:S(2)}) %all-to-all-start.1) | async-done | bytes 1048608 | tf_op jit(solution)/shard_map/all_to_all | solution.py:54
  93.2 0.7 fusion.2
  93.9 0.1 copy.30
  94.0 0.1 reduce_sum.22
  94.1 0.1 fusion.5
  94.2 29.5 %psum.15 = f32[8,8]{1,0:T(8,128)S(1)} all-reduce(f32[8,8]{1,0:T(8,128)S(1)} %fusion.5), channel_id=1, replica_groups=mesh['lat'=16,'lev'=2] {'lat'}, use_global_device_ids=true, to_apply=%region_3.4 | all-reduce | flops 64 | bytes 512 | tf_op jit(solution)/shard_map/psum | solution.py:68
  123.7 0.6 broadcast_multiply_fusion
  124.3 0.6 copy.28
  124.9 1.1 bitcast_multiply_fusion
  (18 shorter events, 0.1 us)
Async XLA Ops:
  0.6 5.5 %copy-start = (bf16[4,1,80,2,1536]{4,3,2,1,0:T(2,128)(2,1)S(1)}, bf16[4,1,80,2,1536]{4,3,2,1,0:T(2,128)(2,1)}, u32[]{:S(2)}) copy-start(bf16[4,1,80,2,1536]{4,3,2,1,0:T(2,128)(2,1)} %param.9) | copy-start | bytes 5898244
  0.6 5.3 %copy-start.6 = (f32[4,1]{0,1:T(1,128)S(1)}, f32[4,1]{0,1:T(1,128)}, u32[]{:S(2)}) copy-start(f32[4,1]{0,1:T(1,128)} %param.12) | copy-start | bytes 52
  0.7 5.3 %copy-start.2 = (f32[4,1,2,1536]{3,2,1,0:T(2,128)S(1)}, f32[4,1,2,1536]{3,2,1,0:T(2,128)}, u32[]{:S(2)}) copy-start(f32[4,1,2,1536]{3,2,1,0:T(2,128)} %param.10) | copy-start | bytes 147460
  0.7 5.3 %copy-start.3 = (f32[4,1,2,1536]{3,2,1,0:T(2,128)S(1)}, f32[4,1,2,1536]{3,2,1,0:T(2,128)}, u32[]{:S(2)}) copy-start(f32[4,1,2,1536]{3,2,1,0:T(2,128)} %param.11) | copy-start | bytes 147460
  0.7 71.9 %all-to-all-start = ((bf16[2,64,40,256]{3,2,1,0:T(8,128)(2,1)}), bf16[2,64,40,256]{3,2,1,0:T(8,128)(2,1)}, u32[]{:S(2)}, u32[]{:S(2)}) async-start(bf16[2,64,40,256]{3,2,1,0:T(8,128)(2,1)} %bitcast.48), calls=%async_computation | async-start | bytes 5242880 | tf_op jit(solution)/shard_map/all_to_all | solution.py:50
  74.9 5.2 %copy-start.5 = (s32[128]{0:T(128)S(1)}, s32[128]{0:T(128)}, u32[]{:S(2)}) copy-start(s32[128]{0:T(128)} %param.16) | copy-start | bytes 1540
  74.9 5.2 %copy-start.7 = (f32[8]{0:T(128)S(1)}, f32[8]{0:T(128)}, u32[]{:S(2)}) copy-start(f32[8]{0:T(128)} %param.17) | copy-start | bytes 100
  74.9 5.3 %copy-start.1 = (f32[128,256]{1,0:T(8,128)S(1)}, f32[128,256]{1,0:T(8,128)}, u32[]{:S(2)}) copy-start(f32[128,256]{1,0:T(8,128)} %param.14) | copy-start | bytes 393220
  75.0 5.3 %copy-start.4 = (s32[128]{0:T(128)S(1)}, s32[128]{0:T(128)}, u32[]{:S(2)}) copy-start(s32[128]{0:T(128)} %param.15) | copy-start | bytes 1540
  76.6 16.6 %all-to-all-start.1 = ((f32[64,16,256]{2,0,1:T(8,128)}), f32[64,16,256]{2,0,1:T(8,128)S(1)}, u32[]{:S(2)}, u32[]{:S(2)}) async-start(f32[64,16,256]{2,0,1:T(8,128)} %copy.26), calls=%async_computation.1 | async-start | bytes 2097152 | tf_op jit(solution)/shard_map/all_to_all | solution.py:54
where the time goes:
time: 126 us
  blocking collectives  95 us (75%)
  waiting for transfers between devices  12.7 us (10%)
  starting transfers between devices  8.74 us (7%)
  local copies, waits for them, and re-layouts  4.43 us (4%)
  other arithmetic  2.83 us (2%)
  matrix products  1.44 us (1%)
    psum x1, blocking collectives, local(): summed = lax.psum(partial_value, ('lat', 'lev'))  65.6 us
    psum x1, blocking collectives, local(): lax.psum(local_totals, 'lat') / math.sqrt(block_total * block_rows / NTYPES)  29.5 us
    all_to_all x1, waiting for transfers between devices, local(): lax.all_to_all(answered[0], 'lev', split_axis=1, concat_axis=0, tiled=True)  12.7 us
    all_to_all x1, starting transfers between devices, local(): lax.all_to_all(grouped, 'lev', split_axis=0, concat_axis=2, tiled=True)  5.16 us
    all_to_all x1, starting transfers between devices, local(): lax.all_to_all(answered[0], 'lev', split_axis=1, concat_axis=0, tiled=True)  3.58 us
  transfers between devices with their start and end apart: 2, of which 1 were waited for; matrix products, arithmetic and copies ran while one was open for 1% of the time, Pallas kernels for 0%

commit v1 on v0

--- a/solution.py
+++ b/solution.py
@@ -8,6 +8,7 @@
 LAT0 = 256
 REGIONS = 4
 NTYPES = 8
+_feed_rings = lambda values, across, axis_key: lax.psum(lax.psum(values, across), axis_key)
 
 
 def local(
@@ -36,7 +37,7 @@
     region = lat_index * REGIONS // lat_total
     onehot = (region[None, :] == jnp.arange(REGIONS, dtype=jnp.int32)[:, None]).astype(jnp.float32)
     partial_value = jnp.einsum("vkj,rj->vkr", folded, onehot, precision=lax.Precision.HIGHEST)
-    summed = lax.psum(partial_value, ("lat", "lev"))
+    summed = _feed_rings(partial_value, "lev", axis_key="lat")
     members = anomalies.shape[2]
     norm_scale = math.sqrt(lev_total * lat_total * lon_count / REGIONS)
     weights = (jnp.transpose(summed, (1, 0, 2)).reshape(members, -1) / norm_scale).astype(

time: 126 us -> 124 us (0.984)
  waiting for transfers between devices: 12.7 us -> 10.5 us
    all_to_all x1, waiting for transfers between devices: 12.7 us -> 10.5 us  [local(): lax.all_to_all(answered[0], 'lev', split_axis=1, concat_axis=0, tiled=True)]
    psum x1 -> x2, blocking collectives: 65.6 us -> 64.4 us  [the longest x1 33.4 us: lax.psum(lax.psum(values, across), axis_key)]
where the time goes in v1:
time: 124 us; the launch traced here: 123 us
  blocking collectives  94.5 us (76%)
  waiting for transfers between devices  10.5 us (8%)
  starting transfers between devices  8.73 us (7%)
  local copies, waits for them, and re-layouts  4.43 us (4%)
  other arithmetic  2.83 us (2%)
  matrix products  1.44 us (1%)
    psum x1, blocking collectives, lax.psum(lax.psum(values, across), axis_key)  33.4 us
    psum x1, blocking collectives, lax.psum(values, across)  31.1 us
    psum x1, blocking collectives, local(): lax.psum(local_totals, 'lat') / math.sqrt(block_total * block_rows / NTYPES)  30.1 us
    all_to_all x1, waiting for transfers between devices, local(): lax.all_to_all(answered[0], 'lev', split_axis=1, concat_axis=0, tiled=True)  10.5 us
    all_to_all x1, starting transfers between devices, local(): lax.all_to_all(grouped, 'lev', split_axis=0, concat_axis=2, tiled=True)  5.15 us
    all_to_all x1, starting transfers between devices, local(): lax.all_to_all(answered[0], 'lev', split_axis=1, concat_axis=0, tiled=True)  3.58 us
  transfers between devices with their start and end apart: 2, of which 1 were waited for; matrix products, arithmetic and copies ran while one was open for 1% of the time, Pallas kernels for 0%

profile of v1, /device:TPU:0, one launch (start us, length us, event | category | flops | bytes accessed | tf_op | source)
XLA Modules:
  0.0 123.3 jit_solution(17289023685601091887)
XLA Ops:
  0.6 0.0 copy-start
  0.7 5.1 %all-to-all-start = ((bf16[2,64,40,256]{3,2,1,0:T(8,128)(2,1)}), bf16[2,64,40,256]{3,2,1,0:T(8,128)(2,1)}, u32[]{:S(2)}, u32[]{:S(2)}) async-start(bf16[2,64,40,256]{3,2,1,0:T(8,128)(2,1)} %bitcast.48), calls=%async_computation | async-start | bytes 5242880 | tf_op jit(solution)/shard_map/all_to_all | solution.py:51
  5.9 0.1 broadcast_multiply_fusion.1
  6.0 0.1 fusion.4
  6.1 0.6 fusion
  6.7 0.3 fusion.7
  7.0 31.1 %psum.21 = f32[4,80,4]{1,2,0:T(4,128)S(1)} all-reduce(f32[4,80,4]{1,2,0:T(4,128)S(1)} %fusion.7), channel_id=1, replica_groups=mesh['lat'=16,'lev'=2] {'lev'}, use_global_device_ids=true, to_apply=%region_0.1 | all-reduce | flops 1280 | bytes 10240 | tf_op jit(solution)/shard_map/psum | solution.py:11
  38.0 33.4 %psum.22 = f32[4,80,4]{1,2,0:T(4,128)S(1)} all-reduce(f32[4,80,4]{1,2,0:T(4,128)S(1)} %psum.21), channel_id=1, replica_groups=mesh['lat'=16,'lev'=2] {'lat'}, use_global_device_ids=true, to_apply=%region_1.2 | all-reduce | flops 1280 | bytes 10240 | tf_op jit(solution)/shard_map/psum | solution.py:11
  71.4 1.9 %copy.25 = bf16[1,64,2,40,256]{4,3,2,1,0:T(8,128)(2,1)S(1)} copy(bf16[1,64,2,40,256]{4,3,1,2,0:T(8,128)(2,1)} %bitcast.13) | data formatting | bytes 5242880 | tf_op jit(solution)/shard_map/all_to_all | solution.py:51
  73.4 0.5 convolution_bitcast_fusion
  73.9 1.6 %copy.26 = f32[64,16,256]{2,0,1:T(8,128)} copy(f32[64,16,256]{2,1,0:T(8,128)S(1)} %convolution_bitcast_fusion) | data formatting | bytes 2097152 | tf_op jit(solution)/shard_map/squeeze | solution.py:55
  75.4 3.6 %all-to-all-start.1 = ((f32[64,16,256]{2,0,1:T(8,128)}), f32[64,16,256]{2,0,1:T(8,128)S(1)}, u32[]{:S(2)}, u32[]{:S(2)}) async-start(f32[64,16,256]{2,0,1:T(8,128)} %copy.26), calls=%async_computation.1 | async-start | bytes 2097152 | tf_op jit(solution)/shard_map/all_to_all | solution.py:55
  79.0 0.1 select_reduce_fusion
  79.1 0.1 select_multiply_fusion
  79.2 0.1 copy.29
  79.4 10.5 %all-to-all-done.1 = f32[64,16,256]{2,0,1:T(8,128)S(1)} async-done(((f32[64,16,256]{2,0,1:T(8,128)}), f32[64,16,256]{2,0,1:T(8,128)S(1)}, u32[]{:S(2)}, u32[]{:S(2)}) %all-to-all-start.1) | async-done | bytes 1048608 | tf_op jit(solution)/shard_map/all_to_all | solution.py:55
  89.9 0.7 fusion.2
  90.6 0.1 copy.30
  90.7 0.1 reduce_sum.22
  90.8 0.1 fusion.5
  90.9 30.1 %psum.23 = f32[8,8]{1,0:T(8,128)S(1)} all-reduce(f32[8,8]{1,0:T(8,128)S(1)} %fusion.5), channel_id=1, replica_groups=mesh['lat'=16,'lev'=2] {'lat'}, use_global_device_ids=true, to_apply=%region_4.5 | all-reduce | flops 64 | bytes 512 | tf_op jit(solution)/shard_map/psum | solution.py:69
  121.0 0.6 broadcast_multiply_fusion
  121.6 0.6 copy.28
  122.2 1.1 bitcast_multiply_fusion
  (19 shorter events, 0.1 us)
Async XLA Ops:
  0.6 5.5 %copy-start = (bf16[4,1,80,2,1536]{4,3,2,1,0:T(2,128)(2,1)S(1)}, bf16[4,1,80,2,1536]{4,3,2,1,0:T(2,128)(2,1)}, u32[]{:S(2)}) copy-start(bf16[4,1,80,2,1536]{4,3,2,1,0:T(2,128)(2,1)} %param.9) | copy-start | bytes 5898244
  0.6 5.2 %copy-start.6 = (f32[4,1]{0,1:T(1,128)S(1)}, f32[4,1]{0,1:T(1,128)}, u32[]{:S(2)}) copy-start(f32[4,1]{0,1:T(1,128)} %param.12) | copy-start | bytes 52
  0.7 5.3 %copy-start.2 = (f32[4,1,2,1536]{3,2,1,0:T(2,128)S(1)}, f32[4,1,2,1536]{3,2,1,0:T(2,128)}, u32[]{:S(2)}) copy-start(f32[4,1,2,1536]{3,2,1,0:T(2,128)} %param.10) | copy-start | bytes 147460
  0.7 5.3 %copy-start.3 = (f32[4,1,2,1536]{3,2,1,0:T(2,128)S(1)}, f32[4,1,2,1536]{3,2,1,0:T(2,128)}, u32[]{:S(2)}) copy-start(f32[4,1,2,1536]{3,2,1,0:T(2,128)} %param.11) | copy-start | bytes 147460
  0.7 70.7 %all-to-all-start = ((bf16[2,64,40,256]{3,2,1,0:T(8,128)(2,1)}), bf16[2,64,40,256]{3,2,1,0:T(8,128)(2,1)}, u32[]{:S(2)}, u32[]{:S(2)}) async-start(bf16[2,64,40,256]{3,2,1,0:T(8,128)(2,1)} %bitcast.48), calls=%async_computation | async-start | bytes 5242880 | tf_op jit(solution)/shard_map/all_to_all | solution.py:51
  73.8 5.2 %copy-start.5 = (s32[128]{0:T(128)S(1)}, s32[128]{0:T(128)}, u32[]{:S(2)}) copy-start(s32[128]{0:T(128)} %param.16) | copy-start | bytes 1540
  73.8 5.2 %copy-start.7 = (f32[8]{0:T(128)S(1)}, f32[8]{0:T(128)}, u32[]{:S(2)}) copy-start(f32[8]{0:T(128)} %param.17) | copy-start | bytes 100
  73.8 5.3 %copy-start.1 = (f32[128,256]{1,0:T(8,128)S(1)}, f32[128,256]{1,0:T(8,128)}, u32[]{:S(2)}) copy-start(f32[128,256]{1,0:T(8,128)} %param.14) | copy-start | bytes 393220
  73.8 5.3 %copy-start.4 = (s32[128]{0:T(128)S(1)}, s32[128]{0:T(128)}, u32[]{:S(2)}) copy-start(s32[128]{0:T(128)} %param.15) | copy-start | bytes 1540
  75.4 14.5 %all-to-all-start.1 = ((f32[64,16,256]{2,0,1:T(8,128)}), f32[64,16,256]{2,0,1:T(8,128)S(1)}, u32[]{:S(2)}, u32[]{:S(2)}) async-start(f32[64,16,256]{2,0,1:T(8,128)} %copy.26), calls=%async_computation.1 | async-start | bytes 2097152 | tf_op jit(solution)/shard_map/all_to_all | solution.py:55

commit v2 on v0

--- a/solution.py
+++ b/solution.py
@@ -36,7 +36,8 @@
     region = lat_index * REGIONS // lat_total
     onehot = (region[None, :] == jnp.arange(REGIONS, dtype=jnp.int32)[:, None]).astype(jnp.float32)
     partial_value = jnp.einsum("vkj,rj->vkr", folded, onehot, precision=lax.Precision.HIGHEST)
-    summed = lax.psum(partial_value, ("lat", "lev"))
+    shards = lax.all_gather(partial_value, ("lat", "lev"), axis=0, tiled=False)
+    summed = shards.sum(axis=0)
     members = anomalies.shape[2]
     norm_scale = math.sqrt(lev_total * lat_total * lon_count / REGIONS)
     weights = (jnp.transpose(summed, (1, 0, 2)).reshape(members, -1) / norm_scale).astype(

time: 126 us -> 151 us (1.20)
  blocking collectives: 95 us -> 121 us
  waiting for transfers between devices: 12.7 us -> 10.8 us
    all_gather x0 -> x1, blocking collectives: none -> 91.9 us  [local(): shards = lax.all_gather(partial_value, ('lat', 'lev'), axis=0, tiled=False)]
    psum x1 -> x0, blocking collectives: 65.6 us -> none  [local(): summed = lax.psum(partial_value, ('lat', 'lev'))]
    all_to_all x1, waiting for transfers between devices: 12.7 us -> 10.8 us  [local(): lax.all_to_all(answered[0], 'lev', split_axis=1, concat_axis=0, tiled=True)]
where the time goes in v2:
time: 151 us; the launch traced here: 150 us
  blocking collectives  121 us (80%)
  waiting for transfers between devices  10.8 us (7%)
  starting transfers between devices  8.74 us (6%)
  local copies, waits for them, and re-layouts  4.43 us (3%)
  other arithmetic  2.91 us (2%)
    all_gather x1, blocking collectives, local(): shards = lax.all_gather(partial_value, ('lat', 'lev'), axis=0, tiled=False)  91.9 us
    psum x1, blocking collectives, local(): lax.psum(local_totals, 'lat') / math.sqrt(block_total * block_rows / NTYPES)  29.5 us
    all_to_all x1, waiting for transfers between devices, local(): lax.all_to_all(answered[0], 'lev', split_axis=1, concat_axis=0, tiled=True)  10.8 us
    all_to_all x1, starting transfers between devices, local(): lax.all_to_all(grouped, 'lev', split_axis=0, concat_axis=2, tiled=True)  5.16 us
    all_to_all x1, starting transfers between devices, local(): lax.all_to_all(answered[0], 'lev', split_axis=1, concat_axis=0, tiled=True)  3.58 us
  transfers between devices with their start and end apart: 2, of which 1 were waited for; matrix products, arithmetic and copies ran while one was open for 1% of the time, Pallas kernels for 0%

profile of v2, /device:TPU:0, one launch (start us, length us, event | category | flops | bytes accessed | tf_op | source)
XLA Modules:
  0.0 150.5 jit_solution(16024920354035923288)
XLA Ops:
  0.6 0.0 copy-start
  0.7 5.2 %all-to-all-start = ((bf16[2,64,40,256]{3,2,1,0:T(8,128)(2,1)}), bf16[2,64,40,256]{3,2,1,0:T(8,128)(2,1)}, u32[]{:S(2)}, u32[]{:S(2)}) async-start(bf16[2,64,40,256]{3,2,1,0:T(8,128)(2,1)} %bitcast.49), calls=%async_computation | async-start | bytes 5242880 | tf_op jit(solution)/shard_map/all_to_all | solution.py:51
  5.9 0.1 broadcast_multiply_fusion.1
  6.0 0.1 fusion.4
  6.1 0.6 fusion
  6.7 0.3 fusion.7
  7.0 91.9 %all-gather = f32[128,80,4]{1,2,0:T(4,128)S(1)} all-gather(f32[4,80,4]{1,2,0:T(4,128)S(1)} %fusion.7), channel_id=2, replica_groups=mesh['lat'=16,'lev'=2] {'lat','lev'}, dimensions={0}, use_global_device_ids=true | all-gather | bytes 168960 | tf_op jit(solution)/shard_map/all_gather | solution.py:39
  98.9 0.1 reduce_sum.29
  99.0 1.9 %copy.25 = bf16[1,64,2,40,256]{4,3,2,1,0:T(8,128)(2,1)S(1)} copy(bf16[1,64,2,40,256]{4,3,1,2,0:T(8,128)(2,1)} %bitcast.14) | data formatting | bytes 5242880 | tf_op jit(solution)/shard_map/all_to_all | solution.py:51
  100.9 0.5 convolution_bitcast_fusion
  101.4 1.6 %copy.26 = f32[64,16,256]{2,0,1:T(8,128)} copy(f32[64,16,256]{2,1,0:T(8,128)S(1)} %convolution_bitcast_fusion) | data formatting | bytes 2097152 | tf_op jit(solution)/shard_map/squeeze | solution.py:55
  103.0 3.6 %all-to-all-start.1 = ((f32[64,16,256]{2,0,1:T(8,128)}), f32[64,16,256]{2,0,1:T(8,128)S(1)}, u32[]{:S(2)}, u32[]{:S(2)}) async-start(f32[64,16,256]{2,0,1:T(8,128)} %copy.26), calls=%async_computation.1 | async-start | bytes 2097152 | tf_op jit(solution)/shard_map/all_to_all | solution.py:55
  106.6 0.1 select_reduce_fusion
  106.7 0.1 select_multiply_fusion
  106.8 0.1 copy.29
  106.9 10.8 %all-to-all-done.1 = f32[64,16,256]{2,0,1:T(8,128)S(1)} async-done(((f32[64,16,256]{2,0,1:T(8,128)}), f32[64,16,256]{2,0,1:T(8,128)S(1)}, u32[]{:S(2)}, u32[]{:S(2)}) %all-to-all-start.1) | async-done | bytes 1048608 | tf_op jit(solution)/shard_map/all_to_all | solution.py:55
  117.7 0.7 fusion.2
  118.4 0.1 copy.30
  118.5 0.1 reduce_sum.32
  118.6 0.1 fusion.5
  118.7 29.5 %psum.7 = f32[8,8]{1,0:T(8,128)S(1)} all-reduce(f32[8,8]{1,0:T(8,128)S(1)} %fusion.5), channel_id=1, replica_groups=mesh['lat'=16,'lev'=2] {'lat'}, use_global_device_ids=true, to_apply=%region_3.4 | all-reduce | flops 64 | bytes 512 | tf_op jit(solution)/shard_map/psum | solution.py:69
  148.2 0.6 broadcast_multiply_fusion
  148.8 0.6 copy.28
  149.4 1.1 bitcast_multiply_fusion
  (19 shorter events, 0.1 us)
Async XLA Ops:
  0.6 5.5 %copy-start = (bf16[4,1,80,2,1536]{4,3,2,1,0:T(2,128)(2,1)S(1)}, bf16[4,1,80,2,1536]{4,3,2,1,0:T(2,128)(2,1)}, u32[]{:S(2)}) copy-start(bf16[4,1,80,2,1536]{4,3,2,1,0:T(2,128)(2,1)} %param.9) | copy-start | bytes 5898244
  0.6 5.3 %copy-start.6 = (f32[4,1]{0,1:T(1,128)S(1)}, f32[4,1]{0,1:T(1,128)}, u32[]{:S(2)}) copy-start(f32[4,1]{0,1:T(1,128)} %param.12) | copy-start | bytes 52
  0.7 5.3 %copy-start.2 = (f32[4,1,2,1536]{3,2,1,0:T(2,128)S(1)}, f32[4,1,2,1536]{3,2,1,0:T(2,128)}, u32[]{:S(2)}) copy-start(f32[4,1,2,1536]{3,2,1,0:T(2,128)} %param.10) | copy-start | bytes 147460
  0.7 5.3 %copy-start.3 = (f32[4,1,2,1536]{3,2,1,0:T(2,128)S(1)}, f32[4,1,2,1536]{3,2,1,0:T(2,128)}, u32[]{:S(2)}) copy-start(f32[4,1,2,1536]{3,2,1,0:T(2,128)} %param.11) | copy-start | bytes 147460
  0.7 98.3 %all-to-all-start = ((bf16[2,64,40,256]{3,2,1,0:T(8,128)(2,1)}), bf16[2,64,40,256]{3,2,1,0:T(8,128)(2,1)}, u32[]{:S(2)}, u32[]{:S(2)}) async-start(bf16[2,64,40,256]{3,2,1,0:T(8,128)(2,1)} %bitcast.49), calls=%async_computation | async-start | bytes 5242880 | tf_op jit(solution)/shard_map/all_to_all | solution.py:51
  101.4 5.2 %copy-start.5 = (s32[128]{0:T(128)S(1)}, s32[128]{0:T(128)}, u32[]{:S(2)}) copy-start(s32[128]{0:T(128)} %param.16) | copy-start | bytes 1540
  101.4 5.2 %copy-start.7 = (f32[8]{0:T(128)S(1)}, f32[8]{0:T(128)}, u32[]{:S(2)}) copy-start(f32[8]{0:T(128)} %param.17) | copy-start | bytes 100
  101.4 5.3 %copy-start.1 = (f32[128,256]{1,0:T(8,128)S(1)}, f32[128,256]{1,0:T(8,128)}, u32[]{:S(2)}) copy-start(f32[128,256]{1,0:T(8,128)} %param.14) | copy-start | bytes 393220
  101.4 5.3 %copy-start.4 = (s32[128]{0:T(128)S(1)}, s32[128]{0:T(128)}, u32[]{:S(2)}) copy-start(s32[128]{0:T(128)} %param.15) | copy-start | bytes 1540
  103.0 14.7 %all-to-all-start.1 = ((f32[64,16,256]{2,0,1:T(8,128)}), f32[64,16,256]{2,0,1:T(8,128)S(1)}, u32[]{:S(2)}, u32[]{:S(2)}) async-start(f32[64,16,256]{2,0,1:T(8,128)} %copy.26), calls=%async_computation.1 | async-start | bytes 2097152 | tf_op jit(solution)/shard_map/all_to_all | solution.py:55
